TPU v7x, 32 devices: a whole 2x2x4 slice. The times are simulated.
32 devices in a mesh: grp: 2 (over x), dom: 16 (over z, y, core).
Axes of the slice: x: 2, y: 2, z: 4, core: 2. Of those that a mesh axis runs over, the one named last changes fastest.
Arguments:
- positions: float32 [512, 3, 128], P(('grp', 'dom')), may hold values from 0 to 1
- smoothing: float32 [512, 128], P(('grp', 'dom')), may hold values from 0.35 to 0.55
- energy: float32 [512, 128], P(('grp', 'dom')), may hold values from 0.5 to 2
- mass: float32 [512, 128], P(('grp', 'dom')), may hold values from 0.00390625 to 0.015625
- old_density: float32 [512, 128], P(('grp', 'dom')), may hold values from 1 to 6
- active: int32 [512, 128], P(('grp', 'dom')), may hold values 0 or 1
- pair_list: int32 [512, 2], P(('grp', 'dom')), may hold values from 0 to 15
- export_leaves: int32 [768, 2], P(('grp', 'dom')), may hold values from 0 to 15
- export_route: int32 [768, 1], P(('grp', 'dom')), may hold values from 0 to 14; in each aligned block of 24 rows (0 to 23, 24 to 47, ...) at most 2 rows name the same one
Outputs:
- density: float32 [512, 128], P(('grp', 'dom'))
- acceleration: float32 [512, 3, 128], P(('grp', 'dom'))
- timestep: float32 [], replicated
Inputs may be any that keep to these rules, and one draw needn't show every extreme that they name: `pair_list`: indices of leaf blocks of the domain that holds the row. `export_leaves`: column 0 is a leaf block of the domain that holds the row, column 1 a leaf block of the destination domain. `export_route`: among the rows of one domain no value occurs more than 2 times; in some domains one value occurs exactly 2 times. `active`: every domain holds some particles with value 1.
All inputs are finite; a program needn't handle non-finite values. No bound on the sum of `active` on one device may be relied on, other than what follows from the above.
Results may differ from a plain program's by a relative error of at most 0.0003.
Values sent between devices are 32-bit elements; how exact they have to be, the bound alone decides.
No kernel may reach another device: no remote copies, remote signals or barrier semaphores. Data moves between devices by JAX's collectives and lax.ppermute only.
A program may use at most 64 MiB of HBM per device.

v0:
```python
import math
import jax
import jax.numpy as jnp
from jax import lax
from jax.sharding import PartitionSpec as P

MOST = 2
ADIABATIC = 5.0 / 3.0
COURANT = 0.3
batch_tiles = 8


def kernel_value(dist, smooth):
    ratio = dist / smooth
    inner = 1.0 - 6.0 * ratio * ratio + 6.0 * ratio * ratio * ratio
    remain = jnp.maximum(1.0 - ratio, 0.0)
    outer = 2.0 * remain * remain * remain
    return jnp.where(ratio < 0.5, inner, outer) * (8.0 / math.pi) / (smooth * smooth * smooth)


def kernel_slope(dist, smooth):
    ratio = dist / smooth
    inner = -12.0 + 18.0 * ratio
    remain = jnp.maximum(1.0 - ratio, 0.0)
    outer = -6.0 * remain * remain / jnp.maximum(ratio, 0.5)
    square = smooth * smooth
    return jnp.where(ratio < 0.5, inner, outer) * (8.0 / math.pi) / (square * square * smooth)


def density_tile(own_pos, own_h, far_pos, far_mass):
    offset = own_pos[:, :, None] - far_pos[:, None, :]
    dist = jnp.sqrt(jnp.sum(offset * offset, axis=0))
    return jnp.sum(kernel_value(dist, own_h[:, None]) * far_mass[None, :], axis=1)


def force_tile(own_pos, own_h, own_term, far_pos, far_h, far_mass, far_term):
    offset = own_pos[:, :, None] - far_pos[:, None, :]
    dist = jnp.sqrt(jnp.sum(offset * offset, axis=0))
    slope = 0.5 * (kernel_slope(dist, own_h[:, None]) + kernel_slope(dist, far_h[None, :]))
    weight = far_mass[None, :] * (own_term[:, None] + far_term[None, :]) * slope
    return -jnp.sum(weight[None, :, :] * offset, axis=2)


def blockwise(kernel, operands):
    count = operands[0].shape[0]
    width = min(batch_tiles, count)
    shaped = tuple((item.reshape((count // width, width) + item.shape[1:]) for item in operands))
    result = lax.map(lambda group: jax.vmap(kernel)(*group), shaped)
    return result.reshape((count,) + result.shape[2:])


def collect(owner, values):
    flat = values.reshape(values.shape[0], -1)
    total = jnp.dot(
        owner, flat, precision=lax.Precision.HIGHEST, preferred_element_type=jnp.float32
    )
    return total.reshape((owner.shape[0],) + values.shape[1:])


def body(
    positions, smoothing, energy, mass, old_density, active, pair_list, export_leaves, export_route
):
    leaves = positions.shape[0]
    width = positions.shape[2]
    exported = export_leaves.shape[0]
    domains = lax.axis_size("dom")
    myself = lax.axis_index("dom")
    slots = domains * MOST
    target_dom = (myself + 1 + export_route[:, 0]) % domains
    columns = jnp.arange(domains, dtype=jnp.int32)
    onehot = (target_dom[:, None] == columns[None, :]).astype(jnp.int32)
    earlier = jnp.cumsum(onehot, axis=0) - onehot
    rank_in = jnp.sum(earlier * onehot, axis=1)
    slot_of = target_dom * MOST + rank_in
    match = (slot_of[None, :] == jnp.arange(slots, dtype=jnp.int32)[:, None]).astype(jnp.int32)
    filled = jnp.sum(match, axis=1) > 0
    chosen = jnp.sum(match * jnp.arange(exported, dtype=jnp.int32)[None, :], axis=1)
    send_leaf = export_leaves[chosen, 0]
    send_target = jnp.where(filled, export_leaves[chosen, 1], 0)
    leaf_ids = jnp.arange(leaves, dtype=jnp.int32)
    slot_owner = ((send_leaf[None, :] == leaf_ids[:, None]) & filled[None, :]).astype(jnp.float32)
    pair_owner = (pair_list[None, :, 0] == leaf_ids[:, None]).astype(jnp.float32)
    own_idx = pair_list[:, 0]
    far_idx = pair_list[:, 1]
    send_pos = positions[send_leaf]
    send_h = smoothing[send_leaf]
    wanted = lax.all_to_all(
        send_target.reshape(domains, MOST), "dom", split_axis=0, concat_axis=0, tiled=True
    )
    wanted = wanted.reshape(slots)
    served = jnp.concatenate(
        [positions[wanted], smoothing[wanted][:, None, :], mass[wanted][:, None, :]], axis=1
    )
    fetched = lax.all_to_all(
        served.reshape(domains, MOST, 5, width), "dom", split_axis=0, concat_axis=0, tiled=True
    )
    fetched = fetched.reshape(slots, 5, width)
    remote_density = collect(
        slot_owner, blockwise(density_tile, (send_pos, send_h, fetched[:, 0:3], fetched[:, 4]))
    )
    local_part = blockwise(
        density_tile, (positions[own_idx], smoothing[own_idx], positions[far_idx], mass[far_idx])
    )
    self_term = mass * kernel_value(jnp.zeros_like(smoothing), smoothing)
    summed = collect(pair_owner, local_part) + remote_density
    density = jnp.where(active == 1, self_term + summed, old_density)
    term = (ADIABATIC - 1.0) * energy / density
    far_term = lax.all_to_all(
        term[wanted].reshape(domains, MOST, width), "dom", split_axis=0, concat_axis=0, tiled=True
    )
    far_term = far_term.reshape(slots, width)
    remote_force = blockwise(
        force_tile,
        (
            send_pos,
            send_h,
            term[send_leaf],
            fetched[:, 0:3],
            fetched[:, 3],
            fetched[:, 4],
            far_term,
        ),
    )
    remote_accel = collect(slot_owner, remote_force)
    local_force = blockwise(
        force_tile,
        (
            positions[own_idx],
            smoothing[own_idx],
            term[own_idx],
            positions[far_idx],
            smoothing[far_idx],
            mass[far_idx],
            term[far_idx],
        ),
    )
    accel = collect(pair_owner, local_force) + remote_accel
    acceleration = jnp.where((active == 1)[:, None, :], accel, 0.0)
    speed = jnp.sqrt(ADIABATIC * (ADIABATIC - 1.0) * energy)
    magnitude = jnp.sqrt(jnp.sum(acceleration * acceleration, axis=1))
    step_size = COURANT * smoothing / (speed + jnp.sqrt(smoothing * magnitude))
    local_least = jnp.min(jnp.where(active == 1, step_size, jnp.inf))
    timestep = lax.pmin(local_least, ("grp", "dom"))
    return (density, acceleration, timestep)


def solution(mesh):
    return jax.shard_map(
        body,
        mesh=mesh,
        in_specs=(
            P(("grp", "dom"), None, None),
            P(("grp", "dom"), None),
            P(("grp", "dom"), None),
            P(("grp", "dom"), None),
            P(("grp", "dom"), None),
            P(("grp", "dom"), None),
            P(("grp", "dom"), None),
            P(("grp", "dom"), None),
            P(("grp", "dom"), None),
        ),
        out_specs=(P(("grp", "dom"), None), P(("grp", "dom"), None, None), P()),
        check_vma=False,
    )
```

profile of v0, /device:TPU:0, one launch (start us, length us, event | category | flops | bytes accessed | tf_op | source)
XLA Modules:
  0.0 107.7 jit_solution(8637589466511635926)
XLA Ops:
  0.7 0.7 fusion.71
  1.7 0.7 fusion.70
  2.4 1.4 %gather_fusion.6 = s32[32]{0:T(128)S(1)} fusion(s32[24,2]{0,1:T(2,128)} %param.24, s32[32]{0:T(128)S(1)} %get-tuple-element.380), kind=kCustom, calls=%fused_computation.6 | custom fusion | bytes 512 | tf_op jit(solution)/shard_map/gather | solution.py:79
  3.9 0.7 select_n.140
  4.6 7.4 %all-to-all-start = ((s32[16,1,2]{2,1,0:T(1,128)}), s32[16,1,2]{2,1,0:T(1,128)S(1)}, u32[]{:S(2)}, u32[]{:S(2)}) async-start(s32[16,1,2]{2,1,0:T(1,128)} %bitcast.42), calls=%async_computation | async-start | bytes 16384 | tf_op jit(solution)/shard_map/all_to_all | solution.py:87
  12.1 0.6 gather_fusion
  12.7 0.6 gather_fusion.2
  13.2 0.8 gather_fusion.4
  14.0 0.6 gather_fusion.5
  14.7 0.6 gather_fusion.10
  15.2 0.6 gather_fusion.1
  15.8 0.6 gather_fusion.13
  16.5 0.6 gather_fusion.3
  17.0 2.3 %while.40 = (s32[]{:T(128)}, f32[2,8,128]{2,1,0:T(8,128)S(1)}, f32[2,8,3,128]{3,2,1,0:T(4,128)S(1)}, f32[2,8,3,128]{3,2,1,0:T(4,128)S(1)}, f32[2,8,128]{2,1,0:T(8,128)S(1)}, /*index=5*/f32[2,8,128]{2,1,0:T(8,128)S(1)}, s32[]{:T(128)}) while((s32[]{:T(128)}, f32[2,8,128]{2,1,0:T(8,128)S(1)}, f32[2,8,3,128]{3,2,1,0:T(4,128)S(1)}, ...), condition=%wide.region_3.4_spmd, body=%wide.region_0.0_spmd.sunk | while | flops 3277826 | bytes 1167461 | solution.py:48
  17.1 0.5 multiply_reduce_fusion.5
  17.6 0.6 fusion.88
  18.2 0.5 multiply_reduce_fusion.5
  18.7 0.6 fusion.88
  19.5 0.5 broadcast.587
  20.0 0.7 reduce.3
  20.8 0.6 gather_fusion.9
  21.4 0.6 gather_fusion.8
  22.0 0.6 gather_fusion.7
  22.6 0.7 pad_maximum_fusion
  23.2 6.0 %all-to-all-start.1 = ((f32[16,2,5,128]{3,1,2,0:T(2,128)}), f32[16,2,5,128]{3,1,2,0:T(2,128)S(1)}, u32[]{:S(2)}, u32[]{:S(2)}) async-start(f32[16,2,5,128]{3,1,2,0:T(2,128)} %pad_maximum_fusion), calls=%async_computation.1 | async-start | bytes 163840 | tf_op jit(solution)/shard_map/all_to_all | solution.py:94
  29.3 7.1 %all-to-all-done.1 = f32[16,2,5,128]{3,1,2,0:T(2,128)S(1)} async-done(((f32[16,2,5,128]{3,1,2,0:T(2,128)}), f32[16,2,5,128]{3,1,2,0:T(2,128)S(1)}, u32[]{:S(2)}, u32[]{:S(2)}) %all-to-all-start.1) | async-done | bytes 81952 | tf_op jit(solution)/shard_map/all_to_all | solution.py:94
  36.5 4.6 %while.41 = (s32[]{:T(128)}, f32[4,8,128]{2,1,0:T(8,128)S(1)}, f32[4,8,3,128]{3,2,1,0:T(4,128)S(1)}, f32[4,8,3,128]{3,2,1,0:T(4,128)S(1)}, f32[4,8,128]{2,1,0:T(8,128)S(1)}, /*index=5*/f32[4,8,128]{2,1,0:T(8,128)S(1)}, s32[]{:T(128)}) while((s32[]{:T(128)}, f32[4,8,128]{2,1,0:T(8,128)S(1)}, f32[4,8,3,128]{3,2,1,0:T(4,128)S(1)}, ...), condition=%wide.region_11.12_spmd, body=%wide.region_8.11_spmd.sunk | while | flops 3277826 | bytes 1167461 | solution.py:48
  36.5 0.5 multiply_reduce_fusion.6
  37.0 0.6 fusion.89
  37.7 0.5 multiply_reduce_fusion.6
  38.2 0.6 fusion.89
  38.8 0.5 multiply_reduce_fusion.6
  39.3 0.6 fusion.89
  40.0 0.5 multiply_reduce_fusion.6
  40.5 0.6 fusion.89
  41.1 0.7 multiply_divide_fusion
  41.8 0.6 gather_fusion.11
  42.4 0.6 gather_fusion.12
  42.9 1.2 %gather_fusion.15 = f32[32,128]{1,0:T(8,128)} fusion(f32[16,128]{1,0:T(8,128)S(1)} %get-tuple-element.382, s32[1024]{0:T(1024)S(1)} %pad_clamp_fusion), kind=kCustom, calls=%fused_computation.15 | custom fusion | bytes 32896 | tf_op jit(solution)/shard_map/gather | solution.py:109
  44.1 4.6 %while.42 = (s32[]{:T(128)}, f32[2,8,3,128]{3,2,1,0:T(4,128)S(1)}, f32[2,8,128]{2,1,0:T(8,128)S(1)}, f32[2,8,128]{2,1,0:T(8,128)S(1)}, f32[2,8,128]{2,1,0:T(8,12...) while((s32[]{:T(128)}, f32[2,8,3,128]{3,2,1,0:T(4,128)S(1)}, ...), condition=%wide.region_15.16_spmd, body=%wide.region_12.15_spmd.sunk | while | flops 6297602 | bytes 2318465 | solution.py:48
  44.1 0.5 fusion.90
  44.7 0.8 multiply_multiply_fusion.28
  45.4 1.0 fusion.91
  46.4 0.5 fusion.90
  47.0 0.8 multiply_multiply_fusion.28
  47.8 1.0 fusion.91
  48.7 3.5 %all-to-all-start.2 = ((f32[16,2,128]{2,1,0:T(2,128)}), f32[16,2,128]{2,1,0:T(2,128)S(1)}, u32[]{:S(2)}, u32[]{:S(2)}) async-start(f32[16,2,128]{2,1,0:T(2,128)} %bitcast.61), calls=%async_computation.2 | async-start | bytes 32768 | tf_op jit(solution)/shard_map/all_to_all | solution.py:108
  52.4 0.6 gather_fusion.14
  53.0 5.8 %all-to-all-done.2 = f32[16,2,128]{2,1,0:T(2,128)S(1)} async-done(((f32[16,2,128]{2,1,0:T(2,128)}), f32[16,2,128]{2,1,0:T(2,128)S(1)}, u32[]{:S(2)}, u32[]{:S(2)}) %all-to-all-start.2) | async-done | bytes 16416 | tf_op jit(solution)/shard_map/all_to_all | solution.py:108
  58.7 9.3 %while.43 = (s32[]{:T(128)}, f32[4,8,3,128]{3,2,1,0:T(4,128)S(1)}, f32[4,8,128]{2,1,0:T(8,128)S(1)}, f32[4,8,128]{2,1,0:T(8,128)S(1)}, f32[4,8,128]{2,1,0:T(8,12...) while((s32[]{:T(128)}, f32[4,8,3,128]{3,2,1,0:T(4,128)S(1)}, ...), condition=%wide.region_19.20_spmd, body=%wide.region_16.19_spmd.sunk | while | flops 6297602 | bytes 2318465 | solution.py:48
  58.7 0.5 fusion.92
  59.3 0.8 multiply_multiply_fusion.30
  60.1 1.0 fusion.93
  61.1 0.5 fusion.92
  61.6 0.8 multiply_multiply_fusion.30
  62.4 1.0 fusion.93
  63.4 0.5 fusion.92
  63.9 0.8 multiply_multiply_fusion.30
  64.7 1.0 fusion.93
  66.3 0.8 multiply_multiply_fusion.30
  67.0 1.0 fusion.93
  68.0 0.8 multiply_reduce_fusion.2
  68.8 0.6 select_reduce_fusion.2
  69.4 38.3 %pmin.7 = f32[]{:T(128)} all-reduce(f32[]{:T(128)} %select_reduce_fusion.2), channel_id=1, replica_groups=mesh['grp'=2,'dom'=16] {'grp','dom'}, use_global_device_ids=true, to_apply=%region_22.23 | all-reduce | flops 1 | bytes 8 | tf_op jit(solution)/shard_map/pmin | solution.py:143
  (100 shorter events, 2.1 us)
Async XLA Ops:
  0.6 11.4 %copy-start = (f32[16,3,128]{2,0,1:T(8,128)S(1)}, f32[16,3,128]{2,0,1:T(8,128)}, u32[]{:S(2)}) copy-start(f32[16,3,128]{2,0,1:T(8,128)} %param.17) | copy-start | bytes 73732
  0.6 12.6 %copy-start.1 = (s32[24,2]{0,1:T(2,128)S(1)}, s32[24,2]{0,1:T(2,128)}, u32[]{:S(2)}) copy-start(s32[24,2]{0,1:T(2,128)} %param.24) | copy-start | bytes 580
  0.7 11.4 %copy-start.6 = (s32[16,2]{0,1:T(2,128)S(1)}, s32[16,2]{0,1:T(2,128)}, u32[]{:S(2)}) copy-start(s32[16,2]{0,1:T(2,128)} %param.23) | copy-start | bytes 388
  0.7 12.0 %copy-start.2 = (f32[16,128]{1,0:T(8,128)S(1)}, f32[16,128]{1,0:T(8,128)}, u32[]{:S(2)}) copy-start(f32[16,128]{1,0:T(8,128)} %param.18) | copy-start | bytes 24580
  4.6 14.9 %all-to-all-start = ((s32[16,1,2]{2,1,0:T(1,128)}), s32[16,1,2]{2,1,0:T(1,128)S(1)}, u32[]{:S(2)}, u32[]{:S(2)}) async-start(s32[16,1,2]{2,1,0:T(1,128)} %bitcast.42), calls=%async_computation | async-start | bytes 16384 | tf_op jit(solution)/shard_map/all_to_all | solution.py:87
  14.0 2.4 %copy-start.4 = (s32[16,128]{1,0:T(8,128)S(1)}, s32[16,128]{1,0:T(8,128)}, u32[]{:S(2)}) copy-start(s32[16,128]{1,0:T(8,128)} %param.22) | copy-start | bytes 24580
  14.0 2.4 %copy-start.3 = (f32[16,128]{1,0:T(8,128)S(1)}, f32[16,128]{1,0:T(8,128)}, u32[]{:S(2)}) copy-start(f32[16,128]{1,0:T(8,128)} %param.20) | copy-start | bytes 24580
  23.2 13.1 %all-to-all-start.1 = ((f32[16,2,5,128]{3,1,2,0:T(2,128)}), f32[16,2,5,128]{3,1,2,0:T(2,128)S(1)}, u32[]{:S(2)}, u32[]{:S(2)}) async-start(f32[16,2,5,128]{3,1,2,0:T(2,128)} %pad_maximum_fusion), calls=%async_computation.1 | async-start | bytes 163840 | tf_op jit(solution)/shard_map/all_to_all | solution.py:94
  36.5 4.6 %copy-start.5 = (f32[16,128]{1,0:T(8,128)S(1)}, f32[16,128]{1,0:T(8,128)}, u32[]{:S(2)}) copy-start(f32[16,128]{1,0:T(8,128)} %param.19) | copy-start | bytes 24580
  36.5 4.6 %copy-start.7 = (f32[16,128]{1,0:T(8,128)S(1)}, f32[16,128]{1,0:T(8,128)}, u32[]{:S(2)}) copy-start(f32[16,128]{1,0:T(8,128)} %param.21) | copy-start | bytes 24580
  48.7 10.0 %all-to-all-start.2 = ((f32[16,2,128]{2,1,0:T(2,128)}), f32[16,2,128]{2,1,0:T(2,128)S(1)}, u32[]{:S(2)}, u32[]{:S(2)}) async-start(f32[16,2,128]{2,1,0:T(2,128)} %bitcast.61), calls=%async_computation.2 | async-start | bytes 32768 | tf_op jit(solution)/shard_map/all_to_all | solution.py:108
where the time goes:
time: 108 us
  blocking collectives  38.3 us (35%)
  other arithmetic  23.5 us (22%)
  starting transfers between devices  16.9 us (16%)
  waiting for transfers between devices  12.9 us (12%)
  local copies, waits for them, and re-layouts  12.7 us (12%)
  matrix products  1.74 us (2%)
    pmin x1, blocking collectives, body(): timestep = lax.pmin(local_least, ('grp', 'dom'))  38.3 us
    all_to_all x1, starting transfers between devices, body(): lax.all_to_all(send_target.reshape(domains, MOST), 'dom', split_axis=0, c...  7.41 us
    all_to_all x1, waiting for transfers between devices, body(): lax.all_to_all(served.reshape(domains, MOST, 5, width), 'dom', split_axis...  7.1 us
    all_to_all x1, starting transfers between devices, body(): lax.all_to_all(served.reshape(domains, MOST, 5, width), 'dom', split_axis...  6 us
    all_to_all x1, waiting for transfers between devices, body(): lax.all_to_all(term[wanted].reshape(domains, MOST, width), 'dom', split_a...  5.75 us
    reduce_sum x6, other arithmetic, force_tile(): return -jnp.sum(weight[None, :, :] * offset, axis=2)  5.74 us
    mul x6, other arithmetic, force_tile(): weight = far_mass[None, :] * (own_term[:, None] + far_term[None, :]) * slope  4.61 us
    all_to_all x1, starting transfers between devices, body(): lax.all_to_all(term[wanted].reshape(domains, MOST, width), 'dom', split_a...  3.51 us
  transfers between devices with their start and end apart: 3, of which 2 were waited for; matrix products, arithmetic and copies ran while one was open for 7% of the time, Pallas kernels for 0%

commit v1 on v0

--- a/solution.py
+++ b/solution.py
@@ -84,9 +84,20 @@
     far_idx = pair_list[:, 1]
     send_pos = positions[send_leaf]
     send_h = smoothing[send_leaf]
-    wanted = lax.all_to_all(
-        send_target.reshape(domains, MOST), "dom", split_axis=0, concat_axis=0, tiled=True
-    )
+    x = send_target.reshape(domains, MOST)
+    ways, here = (lax.axis_size("dom"), lax.axis_index("dom"))
+    width_2 = x.shape[0] // ways
+    shape = list(x.shape)
+    shape[0] = width_2
+    height = shape[0]
+    shape[0] = height * ways
+    full = jnp.zeros(shape, x.dtype)
+    for mask in range(ways):
+        part = lax.dynamic_slice_in_dim(x, (here ^ mask) * width_2, width_2, axis=0)
+        if mask:
+            part = lax.ppermute(part, "dom", [(d, d ^ mask) for d in range(ways)])
+        full = lax.dynamic_update_slice_in_dim(full, part, (here ^ mask) * height, axis=0)
+    wanted = full
     wanted = wanted.reshape(slots)
     served = jnp.concatenate(
         [positions[wanted], smoothing[wanted][:, None, :], mass[wanted][:, None, :]], axis=1

time: 108 us -> 123 us (1.14)
  starting transfers between devices: 16.9 us -> 29.7 us
  waiting for transfers between devices: 12.9 us -> 16.4 us
    ppermute x0 -> x15, starting transfers between devices: none -> 22.7 us  [body(): part = lax.ppermute(part, 'dom', [(d, d ^ mask) for d in range(ways)])]
    all_to_all x1 -> x0, starting transfers between devices: 7.41 us -> none  [body(): lax.all_to_all(send_target.reshape(domains, MOST), 'dom', split_axis=0, c...]
    ppermute x0 -> x15, waiting for transfers between devices: none -> 5.47 us  [body(): part = lax.ppermute(part, 'dom', [(d, d ^ mask) for d in range(ways)])]
    all_to_all x1, starting transfers between devices: 6 us -> 3.5 us  [body(): lax.all_to_all(served.reshape(domains, MOST, 5, width), 'dom', split_axis...]
    all_to_all x1, waiting for transfers between devices: 7.1 us -> 5.22 us  [body(): lax.all_to_all(served.reshape(domains, MOST, 5, width), 'dom', split_axis...]
  transfers between devices with their start and end apart: 3 -> 17, of which waited for: 2 -> 4; matrix products, arithmetic and copies ran while one was open for 7% -> 7% of each run, Pallas kernels for 0% -> 0%
where the time goes in v1:
time: 123 us
  blocking collectives  38.3 us (31%)
  starting transfers between devices  29.7 us (24%)
  other arithmetic  22.8 us (19%)
  waiting for transfers between devices  16.4 us (13%)
  local copies, waits for them, and re-layouts  12.2 us (10%)
  matrix products  1.74 us (1%)
    pmin x1, blocking collectives, body(): timestep = lax.pmin(local_least, ('grp', 'dom'))  38.3 us
    ppermute x15, starting transfers between devices, body(): part = lax.ppermute(part, 'dom', [(d, d ^ mask) for d in range(ways)])  22.7 us
    all_to_all x1, waiting for transfers between devices, body(): lax.all_to_all(term[wanted].reshape(domains, MOST, width), 'dom', split_a...  5.75 us
    reduce_sum x6, other arithmetic, force_tile(): return -jnp.sum(weight[None, :, :] * offset, axis=2)  5.74 us
    ppermute x15, waiting for transfers between devices, body(): part = lax.ppermute(part, 'dom', [(d, d ^ mask) for d in range(ways)])  5.47 us
    all_to_all x1, waiting for transfers between devices, body(): lax.all_to_all(served.reshape(domains, MOST, 5, width), 'dom', split_axis...  5.22 us
    mul x6, other arithmetic, force_tile(): weight = far_mass[None, :] * (own_term[:, None] + far_term[None, :]) * slope  4.61 us
    all_to_all x1, starting transfers between devices, body(): lax.all_to_all(term[wanted].reshape(domains, MOST, width), 'dom', split_a...  3.51 us
  transfers between devices with their start and end apart: 17, of which 4 were waited for; matrix products, arithmetic and copies ran while one was open for 7% of the time, Pallas kernels for 0%

profile of v1, /device:TPU:0, one launch (start us, length us, event | category | flops | bytes accessed | tf_op | source)
XLA Modules:
  0.0 123.0 jit_solution(10554858968368105035)
XLA Ops:
  0.7 0.7 fusion.71
  1.7 0.7 fusion.70
  2.5 1.4 %gather_fusion.6 = s32[32]{0:T(128)S(1)} fusion(s32[24,2]{0,1:T(2,128)} %param.24, s32[32]{0:T(128)S(1)} %get-tuple-element.396), kind=kCustom, calls=%fused_computation.6 | custom fusion | bytes 512 | tf_op jit(solution)/shard_map/gather | solution.py:79
  4.1 0.6 collective-permute-start
  4.7 2.6 %collective-permute-start.1 = (s32[1,2]{1,0:T(1,128)S(1)}, s32[1,2]{1,0:T(1,128)S(1)}, u32[]{:S(2)}, u32[]{:S(2)}) collective-permute-start(s32[1,2]{1,0:T(1,128)S(1)} %get-tuple-element.390), channel_id=1, source_target_pairs={{0,2},{1,3},{2,0},{3,1},{4,6},{5,7},{6,4},{7,5},{8,10},{9,11},{10,... | collective-permute-start | bytes 32 | tf_op jit(solution)/shard_map/ppermute | solution.py:98
  7.3 1.8 %collective-permute-start.3 = (s32[1,2]{1,0:T(1,128)S(1)}, s32[1,2]{1,0:T(1,128)S(1)}, u32[]{:S(2)}, u32[]{:S(2)}) collective-permute-start(s32[1,2]{1,0:T(1,128)S(1)} %get-tuple-element.388), channel_id=1, source_target_pairs={{0,4},{1,5},{2,6},{3,7},{4,0},{5,1},{6,2},{7,3},{8,12},{9,13},{10,... | collective-permute-start | bytes 32 | tf_op jit(solution)/shard_map/ppermute | solution.py:98
  9.2 0.6 gather_fusion
  9.8 0.6 gather_fusion.1
  10.4 0.6 gather_fusion.2
  11.0 0.6 gather_fusion.3
  11.6 2.3 %while.40 = (s32[]{:T(128)}, f32[2,8,128]{2,1,0:T(8,128)S(1)}, f32[2,8,3,128]{3,2,1,0:T(4,128)S(1)}, f32[2,8,3,128]{3,2,1,0:T(4,128)S(1)}, f32[2,8,128]{2,1,0:T(8,128)S(1)}, /*index=5*/f32[2,8,128]{2,1,0:T(8,128)S(1)}, s32[]{:T(128)}) while((s32[]{:T(128)}, f32[2,8,128]{2,1,0:T(8,128)S(1)}, f32[2,8,3,128]{3,2,1,0:T(4,128)S(1)}, ...), condition=%wide.region_3.4_spmd, body=%wide.region_0.0_spmd.sunk | while | flops 3277826 | bytes 1167461 | solution.py:48
  11.6 0.5 multiply_reduce_fusion.5
  12.1 0.6 fusion.88
  12.7 0.5 multiply_reduce_fusion.5
  13.3 0.6 fusion.88
  13.9 0.8 gather_fusion.4
  14.8 2.7 %collective-permute-start.5 = (s32[1,2]{1,0:T(1,128)S(1)}, s32[1,2]{1,0:T(1,128)S(1)}, u32[]{:S(2)}, u32[]{:S(2)}) collective-permute-start(s32[1,2]{1,0:T(1,128)S(1)} %get-tuple-element.386), channel_id=1, source_target_pairs={{0,6},{1,7},{2,4},{3,5},{4,2},{5,3},{6,0},{7,1},{8,14},{9,15},{10,... | collective-permute-start | bytes 32 | tf_op jit(solution)/shard_map/ppermute | solution.py:98
  17.7 2.7 %collective-permute-start.7 = (s32[1,2]{1,0:T(1,128)S(1)}, s32[1,2]{1,0:T(1,128)S(1)}, u32[]{:S(2)}, u32[]{:S(2)}) collective-permute-start(s32[1,2]{1,0:T(1,128)S(1)} %get-tuple-element.384), channel_id=1, source_target_pairs={{0,8},{1,9},{2,10},{3,11},{4,12},{5,13},{6,14},{7,15},{8,0},{9,1},... | collective-permute-start | bytes 32 | tf_op jit(solution)/shard_map/ppermute | solution.py:98
  20.6 3.6 %collective-permute-start.9 = (s32[1,2]{1,0:T(1,128)S(1)}, s32[1,2]{1,0:T(1,128)S(1)}, u32[]{:S(2)}, u32[]{:S(2)}) collective-permute-start(s32[1,2]{1,0:T(1,128)S(1)} %get-tuple-element.382), channel_id=1, source_target_pairs={{0,10},{1,11},{2,8},{3,9},{4,14},{5,15},{6,12},{7,13},{8,2},{9,3},... | collective-permute-start | bytes 32 | tf_op jit(solution)/shard_map/ppermute | solution.py:98
  24.4 3.6 %collective-permute-start.11 = (s32[1,2]{1,0:T(1,128)S(1)}, s32[1,2]{1,0:T(1,128)S(1)}, u32[]{:S(2)}, u32[]{:S(2)}) collective-permute-start(s32[1,2]{1,0:T(1,128)S(1)} %get-tuple-element.380), channel_id=1, source_target_pairs={{0,12},{1,13},{2,14},{3,15},{4,8},{5,9},{6,10},{7,11},{8,4},{9,5},... | collective-permute-start | bytes 32 | tf_op jit(solution)/shard_map/ppermute | solution.py:98
  28.1 4.5 %collective-permute-start.13 = (s32[1,2]{1,0:T(1,128)S(1)}, s32[1,2]{1,0:T(1,128)S(1)}, u32[]{:S(2)}, u32[]{:S(2)}) collective-permute-start(s32[1,2]{1,0:T(1,128)S(1)} %get-tuple-element.378), channel_id=1, source_target_pairs={{0,14},{1,15},{2,12},{3,13},{4,10},{5,11},{6,8},{7,9},{8,6},{9,7},... | collective-permute-start | bytes 32 | tf_op jit(solution)/shard_map/ppermute | solution.py:98
  33.0 1.5 %collective-permute-done.13 = s32[1,2]{1,0:T(1,128)S(1)} collective-permute-done((s32[1,2]{1,0:T(1,128)S(1)}, s32[1,2]{1,0:T(1,128)S(1)}, u32[]{:S(2)}, u32[]{:S(2)}) %collective-permute-start.13) | collective-permute-done | bytes 40 | tf_op jit(solution)/shard_map/ppermute | solution.py:98
  34.5 3.9 %collective-permute-done.14 = s32[1,2]{1,0:T(1,128)S(1)} collective-permute-done((s32[1,2]{1,0:T(1,128)S(1)}, s32[1,2]{1,0:T(1,128)S(1)}, u32[]{:S(2)}, u32[]{:S(2)}) %collective-permute-start.14) | collective-permute-done | bytes 40 | tf_op jit(solution)/shard_map/ppermute | solution.py:98
  38.6 0.6 gather_fusion.9
  39.1 0.6 gather_fusion.8
  39.7 0.6 gather_fusion.7
  40.3 0.7 pad_maximum_fusion
  41.0 3.5 %all-to-all-start = ((f32[16,2,5,128]{3,1,2,0:T(2,128)}), f32[16,2,5,128]{3,1,2,0:T(2,128)S(1)}, u32[]{:S(2)}, u32[]{:S(2)}) async-start(f32[16,2,5,128]{3,1,2,0:T(2,128)} %pad_maximum_fusion), calls=%async_computation | async-start | bytes 163840 | tf_op jit(solution)/shard_map/all_to_all | solution.py:105
  44.5 0.6 gather_fusion.13
  45.1 0.6 gather_fusion.5
  45.8 0.6 gather_fusion.10
  46.4 5.2 %all-to-all-done = f32[16,2,5,128]{3,1,2,0:T(2,128)S(1)} async-done(((f32[16,2,5,128]{3,1,2,0:T(2,128)}), f32[16,2,5,128]{3,1,2,0:T(2,128)S(1)}, u32[]{:S(2)}, u32[]{:S(2)}) %all-to-all-start) | async-done | bytes 81952 | tf_op jit(solution)/shard_map/all_to_all | solution.py:105
  51.7 4.6 %while.41 = (s32[]{:T(128)}, f32[4,8,128]{2,1,0:T(8,128)S(1)}, f32[4,8,3,128]{3,2,1,0:T(4,128)S(1)}, f32[4,8,3,128]{3,2,1,0:T(4,128)S(1)}, f32[4,8,128]{2,1,0:T(8,128)S(1)}, /*index=5*/f32[4,8,128]{2,1,0:T(8,128)S(1)}, s32[]{:T(128)}) while((s32[]{:T(128)}, f32[4,8,128]{2,1,0:T(8,128)S(1)}, f32[4,8,3,128]{3,2,1,0:T(4,128)S(1)}, ...), condition=%wide.region_11.12_spmd, body=%wide.region_8.11_spmd.sunk | while | flops 3277826 | bytes 1167461 | solution.py:48
  52.3 0.6 fusion.89
  53.4 0.6 fusion.89
  54.5 0.6 fusion.89
  55.7 0.6 fusion.89
  56.3 0.7 multiply_divide_fusion
  57.0 0.6 gather_fusion.11
  57.6 0.6 gather_fusion.12
  58.2 1.2 gather_fusion.15
  59.3 4.6 %while.42 = (s32[]{:T(128)}, f32[2,8,3,128]{3,2,1,0:T(4,128)S(1)}, f32[2,8,128]{2,1,0:T(8,128)S(1)}, f32[2,8,128]{2,1,0:T(8,128)S(1)}, f32[2,8,128]{2,1,0:T(8,12...) while((s32[]{:T(128)}, f32[2,8,3,128]{3,2,1,0:T(4,128)S(1)}, ...), condition=%wide.region_15.16_spmd, body=%wide.region_12.15_spmd.sunk | while | flops 6297602 | bytes 2318465 | solution.py:48
  59.3 0.5 fusion.90
  59.9 0.8 multiply_multiply_fusion.28
  60.7 1.0 fusion.91
  62.2 0.8 multiply_multiply_fusion.28
  63.0 1.0 fusion.91
  64.0 3.5 %all-to-all-start.1 = ((f32[16,2,128]{2,1,0:T(2,128)}), f32[16,2,128]{2,1,0:T(2,128)S(1)}, u32[]{:S(2)}, u32[]{:S(2)}) async-start(f32[16,2,128]{2,1,0:T(2,128)} %bitcast.60), calls=%async_computation.1 | async-start | bytes 32768 | tf_op jit(solution)/shard_map/all_to_all | solution.py:119
  67.6 0.6 gather_fusion.14
  68.2 5.8 %all-to-all-done.1 = f32[16,2,128]{2,1,0:T(2,128)S(1)} async-done(((f32[16,2,128]{2,1,0:T(2,128)}), f32[16,2,128]{2,1,0:T(2,128)S(1)}, u32[]{:S(2)}, u32[]{:S(2)}) %all-to-all-start.1) | async-done | bytes 16416 | tf_op jit(solution)/shard_map/all_to_all | solution.py:119
  74.0 9.3 %while.43 = (s32[]{:T(128)}, f32[4,8,3,128]{3,2,1,0:T(4,128)S(1)}, f32[4,8,128]{2,1,0:T(8,128)S(1)}, f32[4,8,128]{2,1,0:T(8,128)S(1)}, f32[4,8,128]{2,1,0:T(8,12...) while((s32[]{:T(128)}, f32[4,8,3,128]{3,2,1,0:T(4,128)S(1)}, ...), condition=%wide.region_19.20_spmd, body=%wide.region_16.19_spmd.sunk | while | flops 6297602 | bytes 2318465 | solution.py:48
  74.0 0.5 fusion.92
  74.5 0.8 multiply_multiply_fusion.30
  75.3 1.0 fusion.93
  76.3 0.5 fusion.92
  76.8 0.8 multiply_multiply_fusion.30
  77.6 1.0 fusion.93
  79.2 0.8 multiply_multiply_fusion.30
  79.9 1.0 fusion.93
  81.5 0.8 multiply_multiply_fusion.30
  82.3 1.0 fusion.93
  83.2 0.8 multiply_reduce_fusion.2
  84.0 0.6 select_reduce_fusion.2
  84.6 38.3 %pmin.7 = f32[]{:T(128)} all-reduce(f32[]{:T(128)} %select_reduce_fusion.2), channel_id=1, replica_groups=mesh['grp'=2,'dom'=16] {'grp','dom'}, use_global_device_ids=true, to_apply=%region_22.23 | all-reduce | flops 1 | bytes 8 | tf_op jit(solution)/shard_map/pmin | solution.py:154
  (143 shorter events, 6.2 us)
Async XLA Ops:
  0.6 8.5 %copy-start = (f32[16,3,128]{2,0,1:T(8,128)S(1)}, f32[16,3,128]{2,0,1:T(8,128)}, u32[]{:S(2)}) copy-start(f32[16,3,128]{2,0,1:T(8,128)} %param.17) | copy-start | bytes 73732
  0.6 8.5 %copy-start.4 = (s32[16,128]{1,0:T(8,128)S(1)}, s32[16,128]{1,0:T(8,128)}, u32[]{:S(2)}) copy-start(s32[16,128]{1,0:T(8,128)} %param.22) | copy-start | bytes 24580
  0.7 8.5 %copy-start.6 = (s32[16,2]{0,1:T(2,128)S(1)}, s32[16,2]{0,1:T(2,128)}, u32[]{:S(2)}) copy-start(s32[16,2]{0,1:T(2,128)} %param.23) | copy-start | bytes 388
  3.9 6.5 %copy-start.2 = (f32[16,128]{1,0:T(8,128)S(1)}, f32[16,128]{1,0:T(8,128)}, u32[]{:S(2)}) copy-start(f32[16,128]{1,0:T(8,128)} %param.18) | copy-start | bytes 24580
  3.9 7.1 %copy-start.3 = (f32[16,128]{1,0:T(8,128)S(1)}, f32[16,128]{1,0:T(8,128)}, u32[]{:S(2)}) copy-start(f32[16,128]{1,0:T(8,128)} %param.20) | copy-start | bytes 24580
  4.1 10.6 %collective-permute-start = (s32[1,2]{1,0:T(1,128)S(1)}, s32[1,2]{1,0:T(1,128)S(1)}, u32[]{:S(2)}, u32[]{:S(2)}) collective-permute-start(s32[1,2]{1,0:T(1,128)S(1)} %get-tuple-element.391), channel_id=1, source_target_pairs={{0,1},{1,0},{2,3},{3,2},{4,5},{5,4},{6,7},{7,6},{8,9},{9,8},{10,11... | collective-permute-start | bytes 32 | tf_op jit(solution)/shard_map/ppermute | solution.py:98
  4.7 12.8 %collective-permute-start.1 = (s32[1,2]{1,0:T(1,128)S(1)}, s32[1,2]{1,0:T(1,128)S(1)}, u32[]{:S(2)}, u32[]{:S(2)}) collective-permute-start(s32[1,2]{1,0:T(1,128)S(1)} %get-tuple-element.390), channel_id=1, source_target_pairs={{0,2},{1,3},{2,0},{3,1},{4,6},{5,7},{6,4},{7,5},{8,10},{9,11},{10,... | collective-permute-start | bytes 32 | tf_op jit(solution)/shard_map/ppermute | solution.py:98
  7.3 10.4 %collective-permute-start.2 = (s32[1,2]{1,0:T(1,128)S(1)}, s32[1,2]{1,0:T(1,128)S(1)}, u32[]{:S(2)}, u32[]{:S(2)}) collective-permute-start(s32[1,2]{1,0:T(1,128)S(1)} %get-tuple-element.389), channel_id=1, source_target_pairs={{0,3},{1,2},{2,1},{3,0},{4,7},{5,6},{6,5},{7,4},{8,11},{9,10},{10,... | collective-permute-start | bytes 32 | tf_op jit(solution)/shard_map/ppermute | solution.py:98
  7.3 13.1 %collective-permute-start.3 = (s32[1,2]{1,0:T(1,128)S(1)}, s32[1,2]{1,0:T(1,128)S(1)}, u32[]{:S(2)}, u32[]{:S(2)}) collective-permute-start(s32[1,2]{1,0:T(1,128)S(1)} %get-tuple-element.388), channel_id=1, source_target_pairs={{0,4},{1,5},{2,6},{3,7},{4,0},{5,1},{6,2},{7,3},{8,12},{9,13},{10,... | collective-permute-start | bytes 32 | tf_op jit(solution)/shard_map/ppermute | solution.py:98
  9.1 11.5 %collective-permute-start.4 = (s32[1,2]{1,0:T(1,128)S(1)}, s32[1,2]{1,0:T(1,128)S(1)}, u32[]{:S(2)}, u32[]{:S(2)}) collective-permute-start(s32[1,2]{1,0:T(1,128)S(1)} %get-tuple-element.387), channel_id=1, source_target_pairs={{0,5},{1,4},{2,7},{3,6},{4,1},{5,0},{6,3},{7,2},{8,13},{9,12},{10,... | collective-permute-start | bytes 32 | tf_op jit(solution)/shard_map/ppermute | solution.py:98
  11.6 2.3 %copy-start.1 = (s32[24,2]{0,1:T(2,128)S(1)}, s32[24,2]{0,1:T(2,128)}, u32[]{:S(2)}) copy-start(s32[24,2]{0,1:T(2,128)} %param.24) | copy-start | bytes 580
  14.8 9.4 %collective-permute-start.5 = (s32[1,2]{1,0:T(1,128)S(1)}, s32[1,2]{1,0:T(1,128)S(1)}, u32[]{:S(2)}, u32[]{:S(2)}) collective-permute-start(s32[1,2]{1,0:T(1,128)S(1)} %get-tuple-element.386), channel_id=1, source_target_pairs={{0,6},{1,7},{2,4},{3,5},{4,2},{5,3},{6,0},{7,1},{8,14},{9,15},{10,... | collective-permute-start | bytes 32 | tf_op jit(solution)/shard_map/ppermute | solution.py:98
  17.5 6.8 %collective-permute-start.6 = (s32[1,2]{1,0:T(1,128)S(1)}, s32[1,2]{1,0:T(1,128)S(1)}, u32[]{:S(2)}, u32[]{:S(2)}) collective-permute-start(s32[1,2]{1,0:T(1,128)S(1)} %get-tuple-element.385), channel_id=1, source_target_pairs={{0,7},{1,6},{2,5},{3,4},{4,3},{5,2},{6,1},{7,0},{8,15},{9,14},{10,... | collective-permute-start | bytes 32 | tf_op jit(solution)/shard_map/ppermute | solution.py:98
  17.7 10.3 %collective-permute-start.7 = (s32[1,2]{1,0:T(1,128)S(1)}, s32[1,2]{1,0:T(1,128)S(1)}, u32[]{:S(2)}, u32[]{:S(2)}) collective-permute-start(s32[1,2]{1,0:T(1,128)S(1)} %get-tuple-element.384), channel_id=1, source_target_pairs={{0,8},{1,9},{2,10},{3,11},{4,12},{5,13},{6,14},{7,15},{8,0},{9,1},... | collective-permute-start | bytes 32 | tf_op jit(solution)/shard_map/ppermute | solution.py:98
  20.5 7.7 %collective-permute-start.8 = (s32[1,2]{1,0:T(1,128)S(1)}, s32[1,2]{1,0:T(1,128)S(1)}, u32[]{:S(2)}, u32[]{:S(2)}) collective-permute-start(s32[1,2]{1,0:T(1,128)S(1)} %get-tuple-element.383), channel_id=1, source_target_pairs={{0,9},{1,8},{2,11},{3,10},{4,13},{5,12},{6,15},{7,14},{8,1},{9,0},... | collective-permute-start | bytes 32 | tf_op jit(solution)/shard_map/ppermute | solution.py:98
  20.6 12.1 %collective-permute-start.9 = (s32[1,2]{1,0:T(1,128)S(1)}, s32[1,2]{1,0:T(1,128)S(1)}, u32[]{:S(2)}, u32[]{:S(2)}) collective-permute-start(s32[1,2]{1,0:T(1,128)S(1)} %get-tuple-element.382), channel_id=1, source_target_pairs={{0,10},{1,11},{2,8},{3,9},{4,14},{5,15},{6,12},{7,13},{8,2},{9,3},... | collective-permute-start | bytes 32 | tf_op jit(solution)/shard_map/ppermute | solution.py:98
  24.2 8.6 %collective-permute-start.10 = (s32[1,2]{1,0:T(1,128)S(1)}, s32[1,2]{1,0:T(1,128)S(1)}, u32[]{:S(2)}, u32[]{:S(2)}) collective-permute-start(s32[1,2]{1,0:T(1,128)S(1)} %get-tuple-element.381), channel_id=1, source_target_pairs={{0,11},{1,10},{2,9},{3,8},{4,15},{5,14},{6,13},{7,12},{8,3},{9,2},... | collective-permute-start | bytes 32 | tf_op jit(solution)/shard_map/ppermute | solution.py:98
  24.4 8.5 %collective-permute-start.11 = (s32[1,2]{1,0:T(1,128)S(1)}, s32[1,2]{1,0:T(1,128)S(1)}, u32[]{:S(2)}, u32[]{:S(2)}) collective-permute-start(s32[1,2]{1,0:T(1,128)S(1)} %get-tuple-element.380), channel_id=1, source_target_pairs={{0,12},{1,13},{2,14},{3,15},{4,8},{5,9},{6,10},{7,11},{8,4},{9,5},... | collective-permute-start | bytes 32 | tf_op jit(solution)/shard_map/ppermute | solution.py:98
  28.0 4.9 %collective-permute-start.12 = (s32[1,2]{1,0:T(1,128)S(1)}, s32[1,2]{1,0:T(1,128)S(1)}, u32[]{:S(2)}, u32[]{:S(2)}) collective-permute-start(s32[1,2]{1,0:T(1,128)S(1)} %get-tuple-element.379), channel_id=1, source_target_pairs={{0,13},{1,12},{2,15},{3,14},{4,9},{5,8},{6,11},{7,10},{8,5},{9,4},... | collective-permute-start | bytes 32 | tf_op jit(solution)/shard_map/ppermute | solution.py:98
  28.1 6.3 %collective-permute-start.13 = (s32[1,2]{1,0:T(1,128)S(1)}, s32[1,2]{1,0:T(1,128)S(1)}, u32[]{:S(2)}, u32[]{:S(2)}) collective-permute-start(s32[1,2]{1,0:T(1,128)S(1)} %get-tuple-element.378), channel_id=1, source_target_pairs={{0,14},{1,15},{2,12},{3,13},{4,10},{5,11},{6,8},{7,9},{8,6},{9,7},... | collective-permute-start | bytes 32 | tf_op jit(solution)/shard_map/ppermute | solution.py:98
  32.7 5.8 %collective-permute-start.14 = (s32[1,2]{1,0:T(1,128)S(1)}, s32[1,2]{1,0:T(1,128)S(1)}, u32[]{:S(2)}, u32[]{:S(2)}) collective-permute-start(s32[1,2]{1,0:T(1,128)S(1)} %get-tuple-element.377), channel_id=1, source_target_pairs={{0,15},{1,14},{2,13},{3,12},{4,11},{5,10},{6,9},{7,8},{8,7},{9,6},... | collective-permute-start | bytes 32 | tf_op jit(solution)/shard_map/ppermute | solution.py:98
  41.0 10.6 %all-to-all-start = ((f32[16,2,5,128]{3,1,2,0:T(2,128)}), f32[16,2,5,128]{3,1,2,0:T(2,128)S(1)}, u32[]{:S(2)}, u32[]{:S(2)}) async-start(f32[16,2,5,128]{3,1,2,0:T(2,128)} %pad_maximum_fusion), calls=%async_computation | async-start | bytes 163840 | tf_op jit(solution)/shard_map/all_to_all | solution.py:105
  51.7 4.6 %copy-start.5 = (f32[16,128]{1,0:T(8,128)S(1)}, f32[16,128]{1,0:T(8,128)}, u32[]{:S(2)}) copy-start(f32[16,128]{1,0:T(8,128)} %param.19) | copy-start | bytes 24580
  51.7 4.6 %copy-start.7 = (f32[16,128]{1,0:T(8,128)S(1)}, f32[16,128]{1,0:T(8,128)}, u32[]{:S(2)}) copy-start(f32[16,128]{1,0:T(8,128)} %param.21) | copy-start | bytes 24580
  64.0 10.0 %all-to-all-start.1 = ((f32[16,2,128]{2,1,0:T(2,128)}), f32[16,2,128]{2,1,0:T(2,128)S(1)}, u32[]{:S(2)}, u32[]{:S(2)}) async-start(f32[16,2,128]{2,1,0:T(2,128)} %bitcast.60), calls=%async_computation.1 | async-start | bytes 32768 | tf_op jit(solution)/shard_map/all_to_all | solution.py:119
